TPU v7x, 32 devices: a whole 2x2x4 slice. The times are simulated.
32 devices in a mesh: tm: 8 (over y, x, core), tx: 4 (over z).
Axes of the slice: x: 2, y: 2, z: 4, core: 2. Of those that a mesh axis runs over, the one named last changes fastest.
Arguments:
- state: float32 [8, 64, 256, 128], P('tm', 'tx'), may hold values from -6 to 6
- force: float32 [8, 64, 256, 128], P('tm', 'tx'), may hold values from -6 to 6
- u_init: float32 [64, 256, 128], P('tx'), may hold values from -6 to 6
- kappa: float32 [64, 256], P('tx'), may hold values from 0.1 to 2
- rates: float32 [128], replicated, may hold values from 0.05 to 4
- basis: float32 [128, 128], replicated, may hold values from -1 to 1, as said below
Outputs:
- correction: float32 [8, 64, 256, 128], P('tm', 'tx')
Inputs may be any that keep to these rules, and one draw needn't show every extreme that they name: basis is an orthogonal matrix.
All inputs are finite; a program needn't handle non-finite values.
Results may differ from a plain program's by a relative error of at most 0.0003.
Values sent between devices are 32-bit elements; how exact they have to be, the bound alone decides.
No kernel may reach another device: no remote copies, remote signals or barrier semaphores. Data moves between devices by JAX's collectives and lax.ppermute only.
A program may use at most 64 MiB of HBM per device.

v0:
```python
import math
import jax
import jax.numpy as jnp
from jax import lax
from jax.sharding import PartitionSpec as P

ALPHA = 0.05
TWO_PI = 2.0 * math.pi


def extended(block, sides, width):
    for axis, dim in sides:
        count = lax.axis_size(axis)
        forward = [(i, i + 1) for i in range(count - 1)]
        backward = [(target, source) for source, target in forward]
        low = lax.ppermute(
            lax.slice_in_dim(block, block.shape[dim] - width, None, axis=dim), axis, forward
        )
        high = lax.ppermute(lax.slice_in_dim(block, 0, width, axis=dim), axis, backward)
        block = jnp.concatenate([low, block, high], axis=dim)
    return block


def from_behind(array, axis, by):
    count = lax.axis_size(axis)
    pairs = [(i, i + by) for i in range(count) if 0 <= i + by < count]
    return lax.ppermute(array, axis, pairs)


def neighbours(padded):
    return (
        padded[..., 2:, 1:-1, :]
        + padded[..., :-2, 1:-1, :]
        + padded[..., 1:-1, 2:, :]
        + padded[..., 1:-1, :-2, :]
    )


def relax(source, kappa_b, real_den, imag_den, rims):
    magnitude = real_den * real_den + imag_den * imag_den

    def divide(numer):
        return jnp.stack(
            [
                (numer[0] * real_den + numer[1] * imag_den) / magnitude,
                (numer[1] * real_den - numer[0] * imag_den) / magnitude,
            ]
        )

    field = divide(source)
    for repeat in range(2):
        field = divide(source + kappa_b * rims(field))
    return field


def cell_rims(field):
    padded = extended(field, (("tm", 3), ("tx", 2)), 1)
    return neighbours(padded)


def on_device(state, force, u_init, kappa, rates, basis):
    highest = lax.Precision.HIGHEST
    column_size = state.shape[3]
    steps_total = lax.axis_size("tm")
    here = lax.axis_index("tm")
    earlier = from_behind(state, "tm", 1)
    earlier = jnp.where(here == 0, u_init[None], earlier)
    padded = extended(state, (("tx", 1),), 1)
    padded = jnp.pad(padded, ((0, 0), (0, 0), (1, 1), (0, 0)))
    beside_all = neighbours(padded)
    coords = jnp.dot(state.reshape(-1, column_size), basis, precision=highest)
    vertical = jnp.dot(coords * rates, basis.T, precision=highest).reshape(state.shape)
    kappa_b = kappa[None, :, :, None]
    residual = (
        force
        - (state - earlier)
        - vertical
        - kappa_b * (4.0 * state - beside_all)
        - 0.5 * state**3 / (1.0 + state * state)
    )
    modal = jnp.dot(residual.reshape(-1, column_size), basis, precision=highest).reshape(
        state.shape
    )
    decay = jnp.log(ALPHA) / steps_total
    scaled = modal * jnp.exp(decay * here.astype(jnp.float32))
    gathered = lax.all_to_all(scaled, "tm", split_axis=2, concat_axis=0, tiled=True)
    block_y = gathered.shape[2]
    indices = jnp.arange(steps_total)
    steps_f = indices.astype(jnp.float32)
    products = (indices[:, None] * indices[None, :] % steps_total).astype(jnp.float32)
    angles = TWO_PI * products / steps_total
    cosine = jnp.cos(angles)
    sine = jnp.sin(angles)
    flat_cells = gathered.reshape(steps_total, -1)
    spectrum = jnp.stack(
        [
            jnp.dot(cosine, flat_cells, precision=highest),
            -jnp.dot(sine, flat_cells, precision=highest),
        ]
    ).reshape((2,) + gathered.shape)
    factor = jnp.exp(decay)
    theta = TWO_PI * steps_f / steps_total
    shift_re = 1.0 - factor * jnp.cos(theta)
    shift_im = factor * jnp.sin(theta)
    start = here * block_y
    kappa_cells = lax.dynamic_slice_in_dim(kappa, start, block_y, 1)[None, :, :, None]
    real_den = shift_re[:, None, None, None] + rates + 4.0 * kappa_cells
    imag_den = shift_im[:, None, None, None] + jnp.zeros_like(real_den)
    solved = relax(spectrum, kappa_cells, real_den, imag_den, cell_rims)
    flat_re = solved[0].reshape(steps_total, -1)
    flat_im = solved[1].reshape(steps_total, -1)
    times = (
        jnp.dot(cosine, flat_re, precision=highest) - jnp.dot(sine, flat_im, precision=highest)
    ) / steps_total
    times = times * jnp.exp(-decay * steps_f)[:, None]
    back = lax.all_to_all(
        times.reshape(gathered.shape), "tm", split_axis=0, concat_axis=2, tiled=True
    )
    return jnp.dot(back.reshape(-1, column_size), basis.T, precision=highest).reshape(state.shape)


def solution(mesh):
    return jax.shard_map(
        on_device,
        mesh=mesh,
        in_specs=(
            P("tm", "tx", None, None),
            P("tm", "tx", None, None),
            P("tx", None, None),
            P("tx", None),
            P(),
            P(),
        ),
        out_specs=P("tm", "tx", None, None),
        check_vma=False,
    )
```

profile of v0, /device:TPU:0, one launch (start us, length us, event | category | flops | bytes accessed | tf_op | source)
XLA Modules:
  0.0 164.9 jit_solution(18260656128730488843)
XLA Ops:
  0.0 3.9 %collective-permute-start = (f32[1,16,256,128]{3,2,1,0:T(8,128)}, f32[1,16,256,128]{3,2,1,0:T(8,128)}, u32[]{:S(2)}, u32[]{:S(2)}) collective-permute-start(f32[1,16,256,128]{3,2,1,0:T(8,128)} %param.6), channel_id=1, source_target_pairs={{0,4},{4,8},{8,12},{12,16},{16,20},{20,24},{24,28},{1,5},{5,9},{9,... | collective-permute-start | bytes 6291464 | tf_op jit(solution)/shard_map/ppermute | solution.py:27
  4.9 1.3 collective-permute-start.1
  6.2 4.9 %collective-permute-start.2 = (f32[1,1,256,128]{3,2,1,0:T(8,128)S(1)}, f32[1,1,256,128]{3,2,1,0:T(8,128)S(1)}, u32[]{:S(2)}, u32[]{:S(2)}) collective-permute-start(f32[1,1,256,128]{3,2,1,0:T(8,128)S(1)} %get-tuple-element.21), channel_id=1, source_target_pairs={{0,1},{1,2},{2,3},{4,5},{5,6},{6,7},{8,9},{9,10},{10,11},{12,13},{... | collective-permute-start | bytes 393224 | tf_op jit(solution)/shard_map/ppermute | solution.py:16
  11.1 3.4 %convolution_multiply_fusion = f32[4096,128]{1,0:T(8,128)S(1)} fusion(f32[4096,128]{1,0:T(8,128)} %bitcast.61, f32[128,128]{1,0:T(8,128)S(1)} %copy-done, f32[128]{0:T(128)} %param.10), kind=kOutput, calls=%fused_computation.8 | convolution fusion | flops 805830656 | bytes 4260352 | tf_op jit(solution)/shard_map/dot_general | solution.py:71
  14.6 3.1 %fusion.96 = f32[4096,128]{1,0:T(8,128)} fusion(f32[4096,128]{1,0:T(8,128)S(1)} %convolution_multiply_fusion, f32[128,128]{1,0:T(8,128)S(1)} %copy-done), kind=kOutput, calls=%fused_computation.159 | convolution fusion | flops 805306368 | bytes 4259840 | tf_op jit(solution)/shard_map/dot_general | solution.py:72
  18.0 1.3 copy-done.2
  20.0 4.9 %multiply_bitcast_fusion = f32[1,16,256,128]{3,2,1,0:T(8,128)S(1)} fusion(f32[1,16,256,128]{3,2,1,0:T(8,128)S(1)} %copy-done.1, f32[1,18,258,128]{3,2,1,0:T(8,128)S(1)} %select_maximum_fusion, f32[1,1,256,128]{3,2,1,0:T(8,128)S(1)} %collective-permute-done.2, f32[1,1,256,128]{3,2,1,0:T(8,128)S(1)} %collective-permute-done.1, ...), kind=kOutput, calls=%fused_computation.87 | convolution fusion | flops 815792128 | bytes 17121284 | tf_op jit(solution)/shard_map/dot_general | solution.py:81
  24.9 2.5 %copy.10 = f32[1,16,256,128]{3,1,0,2:T(8,128)} copy(f32[1,16,256,128]{3,2,1,0:T(8,128)S(1)} %multiply_bitcast_fusion) | data formatting | bytes 4194304 | tf_op jit(solution)/shard_map/mul | solution.py:85
  27.4 13.5 %all-to-all-start = ((f32[1,16,256,128]{3,1,0,2:T(8,128)}), f32[1,16,256,128]{3,1,0,2:T(8,128)S(1)}, u32[]{:S(2)}, u32[]{:S(2)}) async-start(f32[1,16,256,128]{3,1,0,2:T(8,128)} %copy.10), calls=%async_computation | async-start | bytes 4194304 | tf_op jit(solution)/shard_map/all_to_all | solution.py:86
  41.2 26.4 %all-to-all-done = f32[1,16,256,128]{3,1,0,2:T(8,128)S(1)} async-done(((f32[1,16,256,128]{3,1,0,2:T(8,128)}), f32[1,16,256,128]{3,1,0,2:T(8,128)S(1)}, u32[]{:S(2)}, u32[]{:S(2)}) %all-to-all-start) | async-done | bytes 2097184 | tf_op jit(solution)/shard_map/all_to_all | solution.py:86
  67.6 1.9 %copy.15 = f32[1,16,8,32,128]{4,3,1,2,0:T(8,128)} copy(f32[1,16,8,32,128]{4,1,3,2,0:T(8,128)S(1)} %bitcast.62) | data formatting | bytes 4194304 | tf_op jit(solution)/shard_map/all_to_all | solution.py:86
  69.5 2.0 %reshape.165 = f32[8,65536]{1,0:T(8,128)S(1)} reshape(f32[8,1,16,32,128]{4,3,2,0,1:T(8,128)} %bitcast.63) | data formatting | bytes 4194304 | tf_op jit(solution)/shard_map/reshape | solution.py:94
  71.5 1.9 %fusion.69 = f32[8,65536]{1,0:T(8,128)S(1)} fusion(f32[8,65536]{1,0:T(8,128)S(1)} %reshape.165), kind=kOutput, calls=%fused_computation.130 | convolution fusion | flops 50332544 | bytes 4194304 | tf_op jit(solution)/shard_map/dot_general | solution.py:97
  73.4 1.9 %convolution_negate_fusion = f32[8,65536]{1,0:T(8,128)S(1)} fusion(f32[8,65536]{1,0:T(8,128)S(1)} %reshape.165), kind=kOutput, calls=%fused_computation.2 | convolution fusion | flops 50856832 | bytes 4194304 | tf_op jit(solution)/shard_map/dot_general | solution.py:98
  76.4 1.3 collective-permute-start.3
  77.7 1.3 collective-permute-start.4
  79.0 2.7 %collective-permute-done.4 = f32[2,8,16,1,128]{4,1,3,2,0:T(8,128)S(1)} collective-permute-done((f32[2,8,16,1,128]{4,1,3,2,0:T(8,128)S(1)}, f32[2,8,16,1,128]{4,1,3,2,0:T(8,128)S(1)}, u32[]{:S(2)}, u32[]{:S(2)}) %collective-permute-start.4) | collective-permute-done | bytes 131104 | tf_op jit(solution)/shard_map/ppermute | solution.py:19
  83.0 4.6 %collective-permute-start.6 = (f32[2,8,1,34,128]{4,1,3,2,0:T(8,128)S(1)}, f32[2,8,1,34,128]{4,1,3,2,0:T(8,128)S(1)}, u32[]{:S(2)}, u32[]{:S(2)}) collective-permute-start(f32[2,8,1,34,128]{4,1,3,2,0:T(8,128)S(1)} %get-tuple-element.10), channel_id=1, source_target_pairs={{0,1},{1,2},{2,3},{4,5},{5,6},{6,7},{8,9},{9,10},{10,11},{12,13},{... | collective-permute-start | bytes 835592 | tf_op jit(solution)/shard_map/ppermute | solution.py:16
  87.6 3.0 %collective-permute-done.5 = f32[2,8,1,34,128]{4,1,3,2,0:T(8,128)S(1)} collective-permute-done((f32[2,8,1,34,128]{4,1,3,2,0:T(8,128)S(1)}, f32[2,8,1,34,128]{4,1,3,2,0:T(8,128)S(1)}, u32[]{:S(2)}, u32[]{:S(2)}) %collective-permute-start.5) | collective-permute-done | bytes 278560 | tf_op jit(solution)/shard_map/ppermute | solution.py:19
  90.6 1.7 %collective-permute-done.6 = f32[2,8,1,34,128]{4,1,3,2,0:T(8,128)S(1)} collective-permute-done((f32[2,8,1,34,128]{4,1,3,2,0:T(8,128)S(1)}, f32[2,8,1,34,128]{4,1,3,2,0:T(8,128)S(1)}, u32[]{:S(2)}, u32[]{:S(2)}) %collective-permute-start.6) | collective-permute-done | bytes 278560 | tf_op jit(solution)/shard_map/ppermute | solution.py:16
  92.3 3.6 %fusion.8 = f32[2,8,16,32,128]{4,1,3,2,0:T(8,128)S(1)} fusion(f32[2,8,16,1,128]{4,1,3,2,0:T(8,128)S(1)} %collective-permute-done.3, f32[1,8,16,32,128]{4,1,3,2,0:T(8,128)S(1)} %get-tuple-element.14, f32[1,8,16,32,128]{4,1,3,2,0:T(8,128)S(1)} %get-tuple-element.13, f32[2,8,16,1,128]{4,1,3,2,0:T(8,128)S(1)} %collective-permute-done.4, ...), kind=kLoop, calls=%fused_computation.29 | loop fusion | flops 18874368 | bytes 13404160 | tf_op jit(solution)/shard_map/add | solution.py:52
  97.0 4.3 %collective-permute-start.7 = (f32[2,8,16,1,128]{4,1,3,2,0:T(8,128)S(1)}, f32[2,8,16,1,128]{4,1,3,2,0:T(8,128)S(1)}, u32[]{:S(2)}, u32[]{:S(2)}) collective-permute-start(f32[2,8,16,1,128]{4,1,3,2,0:T(8,128)S(1)} %get-tuple-element.18), channel_id=1, source_target_pairs={{0,4},{4,8},{8,12},{12,16},{16,20},{20,24},{24,28},{1,5},{5,9},{9,... | collective-permute-start | bytes 393224 | tf_op jit(solution)/shard_map/ppermute | solution.py:16
  102.7 3.3 %collective-permute-done.8 = f32[2,8,16,1,128]{4,1,3,2,0:T(8,128)S(1)} collective-permute-done((f32[2,8,16,1,128]{4,1,3,2,0:T(8,128)S(1)}, f32[2,8,16,1,128]{4,1,3,2,0:T(8,128)S(1)}, u32[]{:S(2)}, u32[]{:S(2)}) %collective-permute-start.8) | collective-permute-done | bytes 131104 | tf_op jit(solution)/shard_map/ppermute | solution.py:19
  106.0 4.4 %collective-permute-start.10 = (f32[2,8,1,34,128]{4,1,3,2,0:T(8,128)S(1)}, f32[2,8,1,34,128]{4,1,3,2,0:T(8,128)S(1)}, u32[]{:S(2)}, u32[]{:S(2)}) collective-permute-start(f32[2,8,1,34,128]{4,1,3,2,0:T(8,128)S(1)} %get-tuple-element.8), channel_id=1, source_target_pairs={{0,1},{1,2},{2,3},{4,5},{5,6},{6,7},{8,9},{9,10},{10,11},{12,13},{... | collective-permute-start | bytes 835592 | tf_op jit(solution)/shard_map/ppermute | solution.py:16
  110.5 1.5 collective-permute-start.9
  112.0 2.9 %collective-permute-done.10 = f32[2,8,1,34,128]{4,1,3,2,0:T(8,128)S(1)} collective-permute-done((f32[2,8,1,34,128]{4,1,3,2,0:T(8,128)S(1)}, f32[2,8,1,34,128]{4,1,3,2,0:T(8,128)S(1)}, u32[]{:S(2)}, u32[]{:S(2)}) %collective-permute-start.10) | collective-permute-done | bytes 278560 | tf_op jit(solution)/shard_map/ppermute | solution.py:16
  114.9 4.7 %collective-permute-done.9 = f32[2,8,1,34,128]{4,1,3,2,0:T(8,128)S(1)} collective-permute-done((f32[2,8,1,34,128]{4,1,3,2,0:T(8,128)S(1)}, f32[2,8,1,34,128]{4,1,3,2,0:T(8,128)S(1)}, u32[]{:S(2)}, u32[]{:S(2)}) %collective-permute-start.9) | collective-permute-done | bytes 278560 | tf_op jit(solution)/shard_map/ppermute | solution.py:19
  119.6 3.6 %fusion.3 = f32[2,8,16,32,128]{4,1,3,2,0:T(8,128)S(1)} fusion(f32[2,8,16,1,128]{4,1,3,2,0:T(8,128)S(1)} %collective-permute-done.7, f32[1,8,16,32,128]{4,1,3,2,0:T(8,128)S(1)} %get-tuple-element.12, f32[1,8,16,32,128]{4,1,3,2,0:T(8,128)S(1)} %get-tuple-element.11, f32[2,8,16,1,128]{4,1,3,2,0:T(8,128)S(1)} %collective-permute-done.8, ...), kind=kLoop, calls=%fused_computation.12 | loop fusion | flops 18874368 | bytes 13404160 | tf_op jit(solution)/shard_map/add | solution.py:52
  123.8 2.2 %fusion.36 = f32[8,65536]{1,0:T(8,128)S(1)} fusion(f32[8,65536]{1,0:T(8,128)S(1)} %bitcast.72, f32[8,65536]{1,0:T(8,128)S(1)} %bitcast.70, f32[8,65536]{1,0:T(8,128)S(1)} %bitcast.67, f32[8]{0:T(128)S(1)} %get-tuple-element.24, f32[8]{0:T(128)S(1)} %get-tuple-element.23, f32[65536]{0:T(1024)S(1)} %bitcast.74), kind=kOutput, calls=%fused_computation.81 | convolution fusion | flops 54002560 | bytes 8650816 | tf_op jit(solution)/shard_map/dot_general | solution.py:113
  126.1 2.4 %fusion = f32[8,65536]{1,0:T(8,128)S(1)} fusion(f32[8,65536]{1,0:T(8,128)S(1)} %fusion.36, f32[8,65536]{1,0:T(8,128)S(1)} %bitcast.71, f32[8,65536]{1,0:T(8,128)S(1)} %bitcast.73, f32[8,65536]{1,0:T(8,128)S(1)} %bitcast.68, f32[8]{0:T(128)S(1)} %exponential_multiply_fusion, f32[8]{0:T(128)S(1)} %get-tuple-element.24, f32[8]{0:T(128)S(1)} %get-tuple-element.23, ...), kind=kOutput, calls=%fused_computation.1 | convolution fusion | flops 55051136 | bytes 10748000 | tf_op jit(solution)/shard_map/dot_general | solution.py:113
  128.9 32.7 %all_to_all.30 = f32[8,16,32,128]{3,2,1,0:T(8,128)S(1)} all-to-all(f32[8,16,32,128]{3,2,1,0:T(8,128)S(1)} %copy.12), channel_id=1, replica_groups=mesh['tm'=8,'tx'=4] {'tm'}, dimensions={0} | all-to-all | bytes 4194304 | tf_op jit(solution)/shard_map/all_to_all | solution.py:116
  161.8 3.1 %convolution_bitcast_fusion = f32[1,16,256,128]{3,2,1,0:T(8,128)} fusion(f32[16,256,128]{2,1,0:T(8,128)S(1)} %bitcast.65, f32[128,128]{1,0:T(8,128)S(1)} %copy-done), kind=kOutput, calls=%fused_computation.91 | convolution fusion | flops 805306368 | bytes 4259840 | tf_op jit(solution)/shard_map/dot_general | solution.py:119
  (36 shorter events, 8.1 us)
Async XLA Ops:
  0.0 11.1 %copy-start = (f32[128,128]{1,0:T(8,128)S(1)}, f32[128,128]{1,0:T(8,128)}, u32[]{:S(2)}) copy-start(f32[128,128]{1,0:T(8,128)} %param.11) | copy-start | bytes 196612
  0.0 18.0 %collective-permute-start = (f32[1,16,256,128]{3,2,1,0:T(8,128)}, f32[1,16,256,128]{3,2,1,0:T(8,128)}, u32[]{:S(2)}, u32[]{:S(2)}) collective-permute-start(f32[1,16,256,128]{3,2,1,0:T(8,128)} %param.6), channel_id=1, source_target_pairs={{0,4},{4,8},{8,12},{12,16},{16,20},{20,24},{24,28},{1,5},{5,9},{9,... | collective-permute-start | bytes 6291464 | tf_op jit(solution)/shard_map/ppermute | solution.py:27
  4.9 12.9 %collective-permute-start.1 = (f32[1,1,256,128]{3,2,1,0:T(8,128)S(1)}, f32[1,1,256,128]{3,2,1,0:T(8,128)S(1)}, u32[]{:S(2)}, u32[]{:S(2)}) collective-permute-start(f32[1,1,256,128]{3,2,1,0:T(8,128)S(1)} %get-tuple-element.22), channel_id=1, source_target_pairs={{1,0},{2,1},{3,2},{5,4},{6,5},{7,6},{9,8},{10,9},{11,10},{13,12},{... | collective-permute-start | bytes 393224 | tf_op jit(solution)/shard_map/ppermute | solution.py:19
  6.2 11.6 %collective-permute-start.2 = (f32[1,1,256,128]{3,2,1,0:T(8,128)S(1)}, f32[1,1,256,128]{3,2,1,0:T(8,128)S(1)}, u32[]{:S(2)}, u32[]{:S(2)}) collective-permute-start(f32[1,1,256,128]{3,2,1,0:T(8,128)S(1)} %get-tuple-element.21), channel_id=1, source_target_pairs={{0,1},{1,2},{2,3},{4,5},{5,6},{6,7},{8,9},{9,10},{10,11},{12,13},{... | collective-permute-start | bytes 393224 | tf_op jit(solution)/shard_map/ppermute | solution.py:16
  14.6 3.2 %copy-start.1 = (f32[1,16,256,128]{3,2,1,0:T(8,128)S(1)}, f32[1,16,256,128]{3,2,1,0:T(8,128)}, u32[]{:S(2)}) copy-start(f32[1,16,256,128]{3,2,1,0:T(8,128)} %param.6) | copy-start | bytes 6291460
  17.7 1.6 copy-start.2
  17.7 1.6 copy-start.3
  17.8 2.2 %copy-start.5 = (f32[1,16,256,128]{3,2,1,0:T(8,128)S(1)}, f32[1,16,256,128]{3,2,1,0:T(8,128)}, u32[]{:S(2)}) copy-start(f32[1,16,256,128]{3,2,1,0:T(8,128)} %param.7) | copy-start | bytes 6291460
  27.4 13.7 %copy-start.4 = (f32[128]{0:T(128)S(1)}, f32[128]{0:T(128)}, u32[]{:S(2)}) copy-start(f32[128]{0:T(128)} %param.10) | copy-start | bytes 1540
  27.4 40.1 %all-to-all-start = ((f32[1,16,256,128]{3,1,0,2:T(8,128)}), f32[1,16,256,128]{3,1,0,2:T(8,128)S(1)}, u32[]{:S(2)}, u32[]{:S(2)}) async-start(f32[1,16,256,128]{3,1,0,2:T(8,128)} %copy.10), calls=%async_computation | async-start | bytes 4194304 | tf_op jit(solution)/shard_map/all_to_all | solution.py:86
  76.4 2.6 %collective-permute-start.3 = (f32[2,8,16,1,128]{4,1,3,2,0:T(8,128)S(1)}, f32[2,8,16,1,128]{4,1,3,2,0:T(8,128)S(1)}, u32[]{:S(2)}, u32[]{:S(2)}) collective-permute-start(f32[2,8,16,1,128]{4,1,3,2,0:T(8,128)S(1)} %get-tuple-element.20), channel_id=1, source_target_pairs={{0,4},{4,8},{8,12},{12,16},{16,20},{20,24},{24,28},{1,5},{5,9},{9,... | collective-permute-start | bytes 393224 | tf_op jit(solution)/shard_map/ppermute | solution.py:16
  77.7 4.0 %collective-permute-start.4 = (f32[2,8,16,1,128]{4,1,3,2,0:T(8,128)S(1)}, f32[2,8,16,1,128]{4,1,3,2,0:T(8,128)S(1)}, u32[]{:S(2)}, u32[]{:S(2)}) collective-permute-start(f32[2,8,16,1,128]{4,1,3,2,0:T(8,128)S(1)} %get-tuple-element.19), channel_id=1, source_target_pairs={{4,0},{8,4},{12,8},{16,12},{20,16},{24,20},{28,24},{5,1},{9,5},{13... | collective-permute-start | bytes 393224 | tf_op jit(solution)/shard_map/ppermute | solution.py:19
  81.7 8.9 %collective-permute-start.5 = (f32[2,8,1,34,128]{4,1,3,2,0:T(8,128)S(1)}, f32[2,8,1,34,128]{4,1,3,2,0:T(8,128)S(1)}, u32[]{:S(2)}, u32[]{:S(2)}) collective-permute-start(f32[2,8,1,34,128]{4,1,3,2,0:T(8,128)S(1)} %get-tuple-element.9), channel_id=1, source_target_pairs={{1,0},{2,1},{3,2},{5,4},{6,5},{7,6},{9,8},{10,9},{11,10},{13,12},{... | collective-permute-start | bytes 835592 | tf_op jit(solution)/shard_map/ppermute | solution.py:19
  83.0 9.3 %collective-permute-start.6 = (f32[2,8,1,34,128]{4,1,3,2,0:T(8,128)S(1)}, f32[2,8,1,34,128]{4,1,3,2,0:T(8,128)S(1)}, u32[]{:S(2)}, u32[]{:S(2)}) collective-permute-start(f32[2,8,1,34,128]{4,1,3,2,0:T(8,128)S(1)} %get-tuple-element.10), channel_id=1, source_target_pairs={{0,1},{1,2},{2,3},{4,5},{5,6},{6,7},{8,9},{9,10},{10,11},{12,13},{... | collective-permute-start | bytes 835592 | tf_op jit(solution)/shard_map/ppermute | solution.py:16
  97.0 5.6 %collective-permute-start.7 = (f32[2,8,16,1,128]{4,1,3,2,0:T(8,128)S(1)}, f32[2,8,16,1,128]{4,1,3,2,0:T(8,128)S(1)}, u32[]{:S(2)}, u32[]{:S(2)}) collective-permute-start(f32[2,8,16,1,128]{4,1,3,2,0:T(8,128)S(1)} %get-tuple-element.18), channel_id=1, source_target_pairs={{0,4},{4,8},{8,12},{12,16},{16,20},{20,24},{24,28},{1,5},{5,9},{9,... | collective-permute-start | bytes 393224 | tf_op jit(solution)/shard_map/ppermute | solution.py:16
  101.4 4.6 %collective-permute-start.8 = (f32[2,8,16,1,128]{4,1,3,2,0:T(8,128)S(1)}, f32[2,8,16,1,128]{4,1,3,2,0:T(8,128)S(1)}, u32[]{:S(2)}, u32[]{:S(2)}) collective-permute-start(f32[2,8,16,1,128]{4,1,3,2,0:T(8,128)S(1)} %get-tuple-element.17), channel_id=1, source_target_pairs={{4,0},{8,4},{12,8},{16,12},{20,16},{24,20},{28,24},{5,1},{9,5},{13... | collective-permute-start | bytes 393224 | tf_op jit(solution)/shard_map/ppermute | solution.py:19
  106.0 8.9 %collective-permute-start.10 = (f32[2,8,1,34,128]{4,1,3,2,0:T(8,128)S(1)}, f32[2,8,1,34,128]{4,1,3,2,0:T(8,128)S(1)}, u32[]{:S(2)}, u32[]{:S(2)}) collective-permute-start(f32[2,8,1,34,128]{4,1,3,2,0:T(8,128)S(1)} %get-tuple-element.8), channel_id=1, source_target_pairs={{0,1},{1,2},{2,3},{4,5},{5,6},{6,7},{8,9},{9,10},{10,11},{12,13},{... | collective-permute-start | bytes 835592 | tf_op jit(solution)/shard_map/ppermute | solution.py:16
  110.5 9.1 %collective-permute-start.9 = (f32[2,8,1,34,128]{4,1,3,2,0:T(8,128)S(1)}, f32[2,8,1,34,128]{4,1,3,2,0:T(8,128)S(1)}, u32[]{:S(2)}, u32[]{:S(2)}) collective-permute-start(f32[2,8,1,34,128]{4,1,3,2,0:T(8,128)S(1)} %get-tuple-element.7), channel_id=1, source_target_pairs={{1,0},{2,1},{3,2},{5,4},{6,5},{7,6},{9,8},{10,9},{11,10},{13,12},{... | collective-permute-start | bytes 835592 | tf_op jit(solution)/shard_map/ppermute | solution.py:19
where the time goes:
time: 166 us; the launch traced here: 165 us
  waiting for transfers between devices  44.7 us (27%)
  starting transfers between devices  43.6 us (26%)
  blocking collectives  32.7 us (20%)
  matrix products  23 us (14%)
  local copies, waits for them, and re-layouts  10.7 us (6%)
  other arithmetic  9.89 us (6%)
    all_to_all x1, blocking collectives, on_device(): lax.all_to_all(times.reshape(gathered.shape), 'tm', split_axis=0, concat_...  32.7 us
    all_to_all x1, waiting for transfers between devices, on_device(): lax.all_to_all(scaled, 'tm', split_axis=2, concat_axis=0, tiled=True)  26.4 us
    ppermute x5, starting transfers between devices, extended(): lax.ppermute(lax.slice_in_dim(block, block.shape[dim] - width, None, axis...  19.5 us
    ppermute x5, waiting for transfers between devices, extended(): lax.ppermute(lax.slice_in_dim(block, 0, width, axis=dim), axis, backward)  13.7 us
    all_to_all x1, starting transfers between devices, on_device(): lax.all_to_all(scaled, 'tm', split_axis=2, concat_axis=0, tiled=True)  13.5 us
    add x2, other arithmetic, relax(): field = divide(source + kappa_b * rims(field))  7.25 us
    ppermute x5, starting transfers between devices, extended(): lax.ppermute(lax.slice_in_dim(block, 0, width, axis=dim), axis, backward)  6.68 us
    dot_general x1, matrix products, on_device(): jnp.dot(residual.reshape(-1, column_size), basis, precision=highest)  4.88 us
  transfers between devices with their start and end apart: 12, of which 7 were waited for; matrix products, arithmetic and copies ran while one was open for 5% of the time, Pallas kernels for 0%

commit v1 on v0

--- a/solution.py
+++ b/solution.py
@@ -83,7 +83,12 @@
     )
     decay = jnp.log(ALPHA) / steps_total
     scaled = modal * jnp.exp(decay * here.astype(jnp.float32))
-    gathered = lax.all_to_all(scaled, "tm", split_axis=2, concat_axis=0, tiled=True)
+    gathered = jnp.concatenate(
+        lax.all_to_all(
+            jnp.stack(jnp.split(scaled, lax.axis_size("tm"), axis=2), axis=0), "tm", 0, 0
+        ),
+        axis=0,
+    )
     block_y = gathered.shape[2]
     indices = jnp.arange(steps_total)
     steps_f = indices.astype(jnp.float32)

time: 166 us -> 167 us (level)
  matrix products: 23 us -> 24.9 us
    unnamed x12 -> x19, local copies, waits for them, and re-layouts: 2 us -> 7.07 us
    mul x1 -> x0, local copies, waits for them, and re-layouts: 2.54 us -> none  [on_device(): scaled = modal * jnp.exp(decay * here.astype(jnp.float32))]
    reshape x1 -> x0, local copies, waits for them, and re-layouts: 1.97 us -> none  [on_device(): flat_cells = gathered.reshape(steps_total, -1)]
    all_to_all x1 -> x0, local copies, waits for them, and re-layouts: 1.95 us -> none  [on_device(): lax.all_to_all(scaled, 'tm', split_axis=2, concat_axis=0, tiled=True)]
where the time goes in v1:
time: 167 us; the launch traced here: 166 us
  waiting for transfers between devices  44.7 us (27%)
  starting transfers between devices  43.6 us (26%)
  blocking collectives  32.7 us (20%)
  matrix products  24.9 us (15%)
  local copies, waits for them, and re-layouts  10 us (6%)
  other arithmetic  9.89 us (6%)
    all_to_all x1, blocking collectives, on_device(): lax.all_to_all(times.reshape(gathered.shape), 'tm', split_axis=0, concat_...  32.7 us
    all_to_all x1, waiting for transfers between devices, on_device(): lax.all_to_all(jnp.stack(jnp.split(scaled, lax.axis_size('tm'), axis=2),...  26.4 us
    ppermute x5, starting transfers between devices, extended(): lax.ppermute(lax.slice_in_dim(block, block.shape[dim] - width, None, axis...  19.5 us
    ppermute x5, waiting for transfers between devices, extended(): lax.ppermute(lax.slice_in_dim(block, 0, width, axis=dim), axis, backward)  13.7 us
    all_to_all x1, starting transfers between devices, on_device(): lax.all_to_all(jnp.stack(jnp.split(scaled, lax.axis_size('tm'), axis=2),...  13.5 us
    add x2, other arithmetic, relax(): field = divide(source + kappa_b * rims(field))  7.25 us
    unnamed x19, local copies, waits for them, and re-layouts  7.07 us
    ppermute x5, starting transfers between devices, extended(): lax.ppermute(lax.slice_in_dim(block, 0, width, axis=dim), axis, backward)  6.68 us
  transfers between devices with their start and end apart: 12, of which 7 were waited for; matrix products, arithmetic and copies ran while one was open for 5% of the time, Pallas kernels for 0%

profile of v1, /device:TPU:0, one launch (start us, length us, event | category | flops | bytes accessed | tf_op | source)
XLA Modules:
  0.0 166.2 jit_solution(3277758221123391601)
XLA Ops:
  0.0 3.9 %collective-permute-start = (f32[1,16,256,128]{3,2,1,0:T(8,128)}, f32[1,16,256,128]{3,2,1,0:T(8,128)}, u32[]{:S(2)}, u32[]{:S(2)}) collective-permute-start(f32[1,16,256,128]{3,2,1,0:T(8,128)} %param.6), channel_id=1, source_target_pairs={{0,4},{4,8},{8,12},{12,16},{16,20},{20,24},{24,28},{1,5},{5,9},{9,... | collective-permute-start | bytes 6291464 | tf_op jit(solution)/shard_map/ppermute | solution.py:27
  4.9 1.3 collective-permute-start.1
  6.2 4.9 %collective-permute-start.2 = (f32[1,1,256,128]{3,2,1,0:T(8,128)S(1)}, f32[1,1,256,128]{3,2,1,0:T(8,128)S(1)}, u32[]{:S(2)}, u32[]{:S(2)}) collective-permute-start(f32[1,1,256,128]{3,2,1,0:T(8,128)S(1)} %get-tuple-element.21), channel_id=1, source_target_pairs={{0,1},{1,2},{2,3},{4,5},{5,6},{6,7},{8,9},{9,10},{10,11},{12,13},{... | collective-permute-start | bytes 393224 | tf_op jit(solution)/shard_map/ppermute | solution.py:16
  11.1 3.4 %convolution_multiply_fusion = f32[4096,128]{1,0:T(8,128)S(1)} fusion(f32[4096,128]{1,0:T(8,128)} %bitcast.92, f32[128,128]{1,0:T(8,128)S(1)} %copy-done, f32[128]{0:T(128)} %param.10), kind=kOutput, calls=%fused_computation.8 | convolution fusion | flops 805830656 | bytes 4260352 | tf_op jit(solution)/shard_map/dot_general | solution.py:71
  14.6 3.1 %fusion.108 = f32[4096,128]{1,0:T(8,128)} fusion(f32[4096,128]{1,0:T(8,128)S(1)} %convolution_multiply_fusion, f32[128,128]{1,0:T(8,128)S(1)} %copy-done), kind=kOutput, calls=%fused_computation.178 | convolution fusion | flops 805306368 | bytes 4259840 | tf_op jit(solution)/shard_map/dot_general | solution.py:72
  18.0 1.3 copy-done.2
  20.0 4.9 %multiply_bitcast_fusion = f32[1,16,256,128]{3,2,1,0:T(8,128)S(1)} fusion(f32[1,16,256,128]{3,2,1,0:T(8,128)S(1)} %copy-done.1, f32[1,18,258,128]{3,2,1,0:T(8,128)S(1)} %select_maximum_fusion, f32[1,1,256,128]{3,2,1,0:T(8,128)S(1)} %collective-permute-done.2, f32[1,1,256,128]{3,2,1,0:T(8,128)S(1)} %collective-permute-done.1, ...), kind=kOutput, calls=%fused_computation.89 | convolution fusion | flops 815792128 | bytes 17121284 | tf_op jit(solution)/shard_map/dot_general | solution.py:81
  30.7 13.5 %all-to-all-start = ((f32[8,1,16,32,128]{4,3,2,1,0:T(8,128)}), f32[8,1,16,32,128]{4,3,2,1,0:T(8,128)S(1)}, u32[]{:S(2)}, u32[]{:S(2)}) async-start(f32[8,1,16,32,128]{4,3,2,1,0:T(8,128)} %fusion.63), calls=%async_computation | async-start | bytes 4194304 | tf_op jit(solution)/shard_map/all_to_all | solution.py:87
  44.4 26.4 %all-to-all-done = f32[8,1,16,32,128]{4,3,2,1,0:T(8,128)S(1)} async-done(((f32[8,1,16,32,128]{4,3,2,1,0:T(8,128)}), f32[8,1,16,32,128]{4,3,2,1,0:T(8,128)S(1)}, u32[]{:S(2)}, u32[]{:S(2)}) %all-to-all-start) | async-done | bytes 2097184 | tf_op jit(solution)/shard_map/all_to_all | solution.py:87
  70.8 2.9 %fusion.26 = f32[8,65536]{1,0:T(8,128)S(1)} fusion(f32[1,8,512,128]{3,2,1,0:T(8,128)S(1)} %bitcast.90), kind=kOutput, calls=%fused_computation.65 | convolution fusion | flops 50332544 | bytes 4194304 | tf_op jit(solution)/shard_map/dot_general | solution.py:102
  73.7 2.9 %convolution_negate_fusion = f32[8,65536]{1,0:T(8,128)S(1)} fusion(f32[1,8,512,128]{3,2,1,0:T(8,128)S(1)} %bitcast.91), kind=kOutput, calls=%fused_computation.2 | convolution fusion | flops 50856832 | bytes 4194304 | tf_op jit(solution)/shard_map/dot_general | solution.py:103
  76.6 1.0 fusion.17
  77.7 1.3 collective-permute-start.3
  79.0 1.3 collective-permute-start.4
  80.3 2.7 %collective-permute-done.4 = f32[2,8,16,1,128]{4,1,3,2,0:T(8,128)S(1)} collective-permute-done((f32[2,8,16,1,128]{4,1,3,2,0:T(8,128)S(1)}, f32[2,8,16,1,128]{4,1,3,2,0:T(8,128)S(1)}, u32[]{:S(2)}, u32[]{:S(2)}) %collective-permute-start.4) | collective-permute-done | bytes 131104 | tf_op jit(solution)/shard_map/ppermute | solution.py:19
  83.0 1.3 collective-permute-start.5
  84.3 4.6 %collective-permute-start.6 = (f32[2,8,1,34,128]{4,1,3,2,0:T(8,128)S(1)}, f32[2,8,1,34,128]{4,1,3,2,0:T(8,128)S(1)}, u32[]{:S(2)}, u32[]{:S(2)}) collective-permute-start(f32[2,8,1,34,128]{4,1,3,2,0:T(8,128)S(1)} %get-tuple-element.10), channel_id=1, source_target_pairs={{0,1},{1,2},{2,3},{4,5},{5,6},{6,7},{8,9},{9,10},{10,11},{12,13},{... | collective-permute-start | bytes 835592 | tf_op jit(solution)/shard_map/ppermute | solution.py:16
  88.9 3.0 %collective-permute-done.5 = f32[2,8,1,34,128]{4,1,3,2,0:T(8,128)S(1)} collective-permute-done((f32[2,8,1,34,128]{4,1,3,2,0:T(8,128)S(1)}, f32[2,8,1,34,128]{4,1,3,2,0:T(8,128)S(1)}, u32[]{:S(2)}, u32[]{:S(2)}) %collective-permute-start.5) | collective-permute-done | bytes 278560 | tf_op jit(solution)/shard_map/ppermute | solution.py:19
  91.9 1.7 %collective-permute-done.6 = f32[2,8,1,34,128]{4,1,3,2,0:T(8,128)S(1)} collective-permute-done((f32[2,8,1,34,128]{4,1,3,2,0:T(8,128)S(1)}, f32[2,8,1,34,128]{4,1,3,2,0:T(8,128)S(1)}, u32[]{:S(2)}, u32[]{:S(2)}) %collective-permute-start.6) | collective-permute-done | bytes 278560 | tf_op jit(solution)/shard_map/ppermute | solution.py:16
  93.6 3.6 %fusion.8 = f32[2,8,16,32,128]{4,1,3,2,0:T(8,128)S(1)} fusion(f32[2,8,16,1,128]{4,1,3,2,0:T(8,128)S(1)} %collective-permute-done.3, f32[1,8,16,32,128]{4,1,3,2,0:T(8,128)S(1)} %get-tuple-element.14, f32[1,8,16,32,128]{4,1,3,2,0:T(8,128)S(1)} %get-tuple-element.13, f32[2,8,16,1,128]{4,1,3,2,0:T(8,128)S(1)} %collective-permute-done.4, ...), kind=kLoop, calls=%fused_computation.29 | loop fusion | flops 18874368 | bytes 13404160 | tf_op jit(solution)/shard_map/add | solution.py:52
  98.3 4.3 %collective-permute-start.7 = (f32[2,8,16,1,128]{4,1,3,2,0:T(8,128)S(1)}, f32[2,8,16,1,128]{4,1,3,2,0:T(8,128)S(1)}, u32[]{:S(2)}, u32[]{:S(2)}) collective-permute-start(f32[2,8,16,1,128]{4,1,3,2,0:T(8,128)S(1)} %get-tuple-element.18), channel_id=1, source_target_pairs={{0,4},{4,8},{8,12},{12,16},{16,20},{20,24},{24,28},{1,5},{5,9},{9,... | collective-permute-start | bytes 393224 | tf_op jit(solution)/shard_map/ppermute | solution.py:16
  102.7 1.3 collective-permute-start.8
  104.0 3.3 %collective-permute-done.8 = f32[2,8,16,1,128]{4,1,3,2,0:T(8,128)S(1)} collective-permute-done((f32[2,8,16,1,128]{4,1,3,2,0:T(8,128)S(1)}, f32[2,8,16,1,128]{4,1,3,2,0:T(8,128)S(1)}, u32[]{:S(2)}, u32[]{:S(2)}) %collective-permute-start.8) | collective-permute-done | bytes 131104 | tf_op jit(solution)/shard_map/ppermute | solution.py:19
  107.3 4.4 %collective-permute-start.10 = (f32[2,8,1,34,128]{4,1,3,2,0:T(8,128)S(1)}, f32[2,8,1,34,128]{4,1,3,2,0:T(8,128)S(1)}, u32[]{:S(2)}, u32[]{:S(2)}) collective-permute-start(f32[2,8,1,34,128]{4,1,3,2,0:T(8,128)S(1)} %get-tuple-element.8), channel_id=1, source_target_pairs={{0,1},{1,2},{2,3},{4,5},{5,6},{6,7},{8,9},{9,10},{10,11},{12,13},{... | collective-permute-start | bytes 835592 | tf_op jit(solution)/shard_map/ppermute | solution.py:16
  111.8 1.5 collective-permute-start.9
  113.3 2.9 %collective-permute-done.10 = f32[2,8,1,34,128]{4,1,3,2,0:T(8,128)S(1)} collective-permute-done((f32[2,8,1,34,128]{4,1,3,2,0:T(8,128)S(1)}, f32[2,8,1,34,128]{4,1,3,2,0:T(8,128)S(1)}, u32[]{:S(2)}, u32[]{:S(2)}) %collective-permute-start.10) | collective-permute-done | bytes 278560 | tf_op jit(solution)/shard_map/ppermute | solution.py:16
  116.2 4.7 %collective-permute-done.9 = f32[2,8,1,34,128]{4,1,3,2,0:T(8,128)S(1)} collective-permute-done((f32[2,8,1,34,128]{4,1,3,2,0:T(8,128)S(1)}, f32[2,8,1,34,128]{4,1,3,2,0:T(8,128)S(1)}, u32[]{:S(2)}, u32[]{:S(2)}) %collective-permute-start.9) | collective-permute-done | bytes 278560 | tf_op jit(solution)/shard_map/ppermute | solution.py:19
  120.9 3.6 %fusion.3 = f32[2,8,16,32,128]{4,1,3,2,0:T(8,128)S(1)} fusion(f32[2,8,16,1,128]{4,1,3,2,0:T(8,128)S(1)} %collective-permute-done.7, f32[1,8,16,32,128]{4,1,3,2,0:T(8,128)S(1)} %get-tuple-element.12, f32[1,8,16,32,128]{4,1,3,2,0:T(8,128)S(1)} %get-tuple-element.11, f32[2,8,16,1,128]{4,1,3,2,0:T(8,128)S(1)} %collective-permute-done.8, ...), kind=kLoop, calls=%fused_computation.12 | loop fusion | flops 18874368 | bytes 13404160 | tf_op jit(solution)/shard_map/add | solution.py:52
  125.1 2.2 %fusion.39 = f32[8,65536]{1,0:T(8,128)S(1)} fusion(f32[8,65536]{1,0:T(8,128)S(1)} %bitcast.101, f32[8,65536]{1,0:T(8,128)S(1)} %bitcast.99, f32[8,65536]{1,0:T(8,128)S(1)} %bitcast.96, f32[8]{0:T(128)S(1)} %get-tuple-element.24, f32[8]{0:T(128)S(1)} %get-tuple-element.23, f32[65536]{0:T(1024)S(1)} %bitcast.103), kind=kOutput, calls=%fused_computation.83 | convolution fusion | flops 54002560 | bytes 8650816 | tf_op jit(solution)/shard_map/dot_general | solution.py:118
  127.4 2.4 %fusion = f32[8,65536]{1,0:T(8,128)S(1)} fusion(f32[8,65536]{1,0:T(8,128)S(1)} %fusion.39, f32[8,65536]{1,0:T(8,128)S(1)} %bitcast.100, f32[8,65536]{1,0:T(8,128)S(1)} %bitcast.102, f32[8,65536]{1,0:T(8,128)S(1)} %bitcast.97, f32[8]{0:T(128)S(1)} %exponential_multiply_fusion, f32[8]{0:T(128)S(1)} %get-tuple-element.24, f32[8]{0:T(128)S(1)} %get-tuple-element.23, ...), kind=kOutput, calls=%fused_computation.1 | convolution fusion | flops 55051136 | bytes 10748000 | tf_op jit(solution)/shard_map/dot_general | solution.py:118
  130.2 32.7 %all_to_all.20 = f32[8,16,32,128]{3,2,1,0:T(8,128)S(1)} all-to-all(f32[8,16,32,128]{3,2,1,0:T(8,128)S(1)} %copy.8), channel_id=1, replica_groups=mesh['tm'=8,'tx'=4] {'tm'}, dimensions={0} | all-to-all | bytes 4194304 | tf_op jit(solution)/shard_map/all_to_all | solution.py:121
  163.1 3.1 %convolution_bitcast_fusion = f32[1,16,256,128]{3,2,1,0:T(8,128)} fusion(f32[16,256,128]{2,1,0:T(8,128)S(1)} %bitcast.94, f32[128,128]{1,0:T(8,128)S(1)} %copy-done), kind=kOutput, calls=%fused_computation.95 | convolution fusion | flops 805306368 | bytes 4259840 | tf_op jit(solution)/shard_map/dot_general | solution.py:124
  (41 shorter events, 10.3 us)
Async XLA Ops:
  0.0 11.1 %copy-start = (f32[128,128]{1,0:T(8,128)S(1)}, f32[128,128]{1,0:T(8,128)}, u32[]{:S(2)}) copy-start(f32[128,128]{1,0:T(8,128)} %param.11) | copy-start | bytes 196612
  0.0 18.0 %collective-permute-start = (f32[1,16,256,128]{3,2,1,0:T(8,128)}, f32[1,16,256,128]{3,2,1,0:T(8,128)}, u32[]{:S(2)}, u32[]{:S(2)}) collective-permute-start(f32[1,16,256,128]{3,2,1,0:T(8,128)} %param.6), channel_id=1, source_target_pairs={{0,4},{4,8},{8,12},{12,16},{16,20},{20,24},{24,28},{1,5},{5,9},{9,... | collective-permute-start | bytes 6291464 | tf_op jit(solution)/shard_map/ppermute | solution.py:27
  4.9 12.9 %collective-permute-start.1 = (f32[1,1,256,128]{3,2,1,0:T(8,128)S(1)}, f32[1,1,256,128]{3,2,1,0:T(8,128)S(1)}, u32[]{:S(2)}, u32[]{:S(2)}) collective-permute-start(f32[1,1,256,128]{3,2,1,0:T(8,128)S(1)} %get-tuple-element.22), channel_id=1, source_target_pairs={{1,0},{2,1},{3,2},{5,4},{6,5},{7,6},{9,8},{10,9},{11,10},{13,12},{... | collective-permute-start | bytes 393224 | tf_op jit(solution)/shard_map/ppermute | solution.py:19
  6.2 11.6 %collective-permute-start.2 = (f32[1,1,256,128]{3,2,1,0:T(8,128)S(1)}, f32[1,1,256,128]{3,2,1,0:T(8,128)S(1)}, u32[]{:S(2)}, u32[]{:S(2)}) collective-permute-start(f32[1,1,256,128]{3,2,1,0:T(8,128)S(1)} %get-tuple-element.21), channel_id=1, source_target_pairs={{0,1},{1,2},{2,3},{4,5},{5,6},{6,7},{8,9},{9,10},{10,11},{12,13},{... | collective-permute-start | bytes 393224 | tf_op jit(solution)/shard_map/ppermute | solution.py:16
  14.6 3.2 %copy-start.1 = (f32[1,16,256,128]{3,2,1,0:T(8,128)S(1)}, f32[1,16,256,128]{3,2,1,0:T(8,128)}, u32[]{:S(2)}) copy-start(f32[1,16,256,128]{3,2,1,0:T(8,128)} %param.6) | copy-start | bytes 6291460
  17.7 1.6 copy-start.2
  17.7 1.6 copy-start.3
  17.8 2.2 %copy-start.5 = (f32[1,16,256,128]{3,2,1,0:T(8,128)S(1)}, f32[1,16,256,128]{3,2,1,0:T(8,128)}, u32[]{:S(2)}) copy-start(f32[1,16,256,128]{3,2,1,0:T(8,128)} %param.7) | copy-start | bytes 6291460
  30.7 13.7 %copy-start.4 = (f32[128]{0:T(128)S(1)}, f32[128]{0:T(128)}, u32[]{:S(2)}) copy-start(f32[128]{0:T(128)} %param.10) | copy-start | bytes 1540
  30.7 40.1 %all-to-all-start = ((f32[8,1,16,32,128]{4,3,2,1,0:T(8,128)}), f32[8,1,16,32,128]{4,3,2,1,0:T(8,128)S(1)}, u32[]{:S(2)}, u32[]{:S(2)}) async-start(f32[8,1,16,32,128]{4,3,2,1,0:T(8,128)} %fusion.63), calls=%async_computation | async-start | bytes 4194304 | tf_op jit(solution)/shard_map/all_to_all | solution.py:87
  77.7 2.6 %collective-permute-start.3 = (f32[2,8,16,1,128]{4,1,3,2,0:T(8,128)S(1)}, f32[2,8,16,1,128]{4,1,3,2,0:T(8,128)S(1)}, u32[]{:S(2)}, u32[]{:S(2)}) collective-permute-start(f32[2,8,16,1,128]{4,1,3,2,0:T(8,128)S(1)} %get-tuple-element.20), channel_id=1, source_target_pairs={{0,4},{4,8},{8,12},{12,16},{16,20},{20,24},{24,28},{1,5},{5,9},{9,... | collective-permute-start | bytes 393224 | tf_op jit(solution)/shard_map/ppermute | solution.py:16
  79.0 4.0 %collective-permute-start.4 = (f32[2,8,16,1,128]{4,1,3,2,0:T(8,128)S(1)}, f32[2,8,16,1,128]{4,1,3,2,0:T(8,128)S(1)}, u32[]{:S(2)}, u32[]{:S(2)}) collective-permute-start(f32[2,8,16,1,128]{4,1,3,2,0:T(8,128)S(1)} %get-tuple-element.19), channel_id=1, source_target_pairs={{4,0},{8,4},{12,8},{16,12},{20,16},{24,20},{28,24},{5,1},{9,5},{13... | collective-permute-start | bytes 393224 | tf_op jit(solution)/shard_map/ppermute | solution.py:19
  83.0 8.9 %collective-permute-start.5 = (f32[2,8,1,34,128]{4,1,3,2,0:T(8,128)S(1)}, f32[2,8,1,34,128]{4,1,3,2,0:T(8,128)S(1)}, u32[]{:S(2)}, u32[]{:S(2)}) collective-permute-start(f32[2,8,1,34,128]{4,1,3,2,0:T(8,128)S(1)} %get-tuple-element.9), channel_id=1, source_target_pairs={{1,0},{2,1},{3,2},{5,4},{6,5},{7,6},{9,8},{10,9},{11,10},{13,12},{... | collective-permute-start | bytes 835592 | tf_op jit(solution)/shard_map/ppermute | solution.py:19
  84.3 9.3 %collective-permute-start.6 = (f32[2,8,1,34,128]{4,1,3,2,0:T(8,128)S(1)}, f32[2,8,1,34,128]{4,1,3,2,0:T(8,128)S(1)}, u32[]{:S(2)}, u32[]{:S(2)}) collective-permute-start(f32[2,8,1,34,128]{4,1,3,2,0:T(8,128)S(1)} %get-tuple-element.10), channel_id=1, source_target_pairs={{0,1},{1,2},{2,3},{4,5},{5,6},{6,7},{8,9},{9,10},{10,11},{12,13},{... | collective-permute-start | bytes 835592 | tf_op jit(solution)/shard_map/ppermute | solution.py:16
  98.3 5.6 %collective-permute-start.7 = (f32[2,8,16,1,128]{4,1,3,2,0:T(8,128)S(1)}, f32[2,8,16,1,128]{4,1,3,2,0:T(8,128)S(1)}, u32[]{:S(2)}, u32[]{:S(2)}) collective-permute-start(f32[2,8,16,1,128]{4,1,3,2,0:T(8,128)S(1)} %get-tuple-element.18), channel_id=1, source_target_pairs={{0,4},{4,8},{8,12},{12,16},{16,20},{20,24},{24,28},{1,5},{5,9},{9,... | collective-permute-start | bytes 393224 | tf_op jit(solution)/shard_map/ppermute | solution.py:16
  102.7 4.6 %collective-permute-start.8 = (f32[2,8,16,1,128]{4,1,3,2,0:T(8,128)S(1)}, f32[2,8,16,1,128]{4,1,3,2,0:T(8,128)S(1)}, u32[]{:S(2)}, u32[]{:S(2)}) collective-permute-start(f32[2,8,16,1,128]{4,1,3,2,0:T(8,128)S(1)} %get-tuple-element.17), channel_id=1, source_target_pairs={{4,0},{8,4},{12,8},{16,12},{20,16},{24,20},{28,24},{5,1},{9,5},{13... | collective-permute-start | bytes 393224 | tf_op jit(solution)/shard_map/ppermute | solution.py:19
  107.3 8.9 %collective-permute-start.10 = (f32[2,8,1,34,128]{4,1,3,2,0:T(8,128)S(1)}, f32[2,8,1,34,128]{4,1,3,2,0:T(8,128)S(1)}, u32[]{:S(2)}, u32[]{:S(2)}) collective-permute-start(f32[2,8,1,34,128]{4,1,3,2,0:T(8,128)S(1)} %get-tuple-element.8), channel_id=1, source_target_pairs={{0,1},{1,2},{2,3},{4,5},{5,6},{6,7},{8,9},{9,10},{10,11},{12,13},{... | collective-permute-start | bytes 835592 | tf_op jit(solution)/shard_map/ppermute | solution.py:16
  111.8 9.1 %collective-permute-start.9 = (f32[2,8,1,34,128]{4,1,3,2,0:T(8,128)S(1)}, f32[2,8,1,34,128]{4,1,3,2,0:T(8,128)S(1)}, u32[]{:S(2)}, u32[]{:S(2)}) collective-permute-start(f32[2,8,1,34,128]{4,1,3,2,0:T(8,128)S(1)} %get-tuple-element.7), channel_id=1, source_target_pairs={{1,0},{2,1},{3,2},{5,4},{6,5},{7,6},{9,8},{10,9},{11,10},{13,12},{... | collective-permute-start | bytes 835592 | tf_op jit(solution)/shard_map/ppermute | solution.py:19
